TPU v7x, 16 devices: a whole 2x2x2 slice. The times are simulated.
16 devices in a mesh: task: 4 (over z, y), row: 4 (over x, core).
Axes of the slice: x: 2, y: 2, z: 2, core: 2. Of those that a mesh axis runs over, the one named last changes fastest.
Arguments:
- points: bfloat16 [65536, 768], P(('task', 'row')), parts along dimension 0
- vectors: bfloat16 [65536, 128], P(('task', 'row')), parts along dimension 0
- length_scale: float32 [4], P('task'), parts along dimension 0
- out_scale: float32 [4], P('task'), parts along dimension 0
Outputs:
- output: float32 [65536, 128], P(('task', 'row')), parts along dimension 0
There are 4 independent parts. A program takes and returns all parts, laid end to end along the dimension named above; each array names one.
All inputs are finite; a program needn't handle non-finite values.
Results may differ from a plain program's by a relative error of at most 0.001.
Values are sent between devices in bfloat16 or wider.
A program may use at most 1 GiB of HBM per device.

v0:
```python
import jax
import jax.numpy as jnp
from jax import lax
from jax.sharding import PartitionSpec as P


def solution(mesh):
    n_row = mesh.shape["row"]
    shift_pairs = [(source_idx, (source_idx + 1) % n_row) for source_idx in range(n_row)]

    def kernel_product(x_rows, norm_rows, x_cols, norm_cols, v_cols, length_scale, out_scale):
        gram_mat = jnp.einsum("if,jf->ij", x_rows, x_cols, preferred_element_type=jnp.float32)
        sq_dist = jnp.maximum(norm_rows[:, None] + norm_cols[None, :] - 2.0 * gram_mat, 0.0)
        kern_tile = (out_scale * jnp.exp(-sq_dist / (2.0 * length_scale * length_scale))).astype(jnp.bfloat16)
        return jnp.dot(kern_tile, v_cols, preferred_element_type=jnp.float32)

    def kernel_pass(x_loc, norm_loc, v_loc, length_scale, out_scale):
        own_part = kernel_product(x_loc, norm_loc, x_loc, norm_loc, v_loc, length_scale, out_scale)

        def visit_step(step_idx, loop_state):
            x_vis, v_vis, running = loop_state
            x_vis = lax.ppermute(x_vis, "row", shift_pairs)
            v_vis = lax.ppermute(v_vis, "row", shift_pairs)
            norm_vis = jnp.sum(jnp.square(x_vis.astype(jnp.float32)), axis=1)
            running = running + kernel_product(x_loc, norm_loc, x_vis, norm_vis, v_vis, length_scale, out_scale)
            return x_vis, v_vis, running

        final_state = lax.fori_loop(1, n_row, visit_step, (x_loc, v_loc, own_part))
        return final_state[2]

    def local_program(x_loc, v_loc, length_scale, out_scale):
        norm_loc = jnp.sum(jnp.square(x_loc.astype(jnp.float32)), axis=1)
        first_pass = kernel_pass(x_loc, norm_loc, v_loc, length_scale, out_scale).astype(jnp.bfloat16)
        return kernel_pass(x_loc, norm_loc, first_pass, length_scale, out_scale)

    row_spec = P(("task", "row"), None)
    return jax.shard_map(local_program, mesh=mesh, in_specs=(row_spec, row_spec, P("task"), P("task")), out_specs=row_spec, check_vma=False)
```

profile of v0, /device:TPU:0, one launch (start us, length us, event | category | flops | bytes accessed | tf_op | source)
XLA Modules:
  0.0 952.5 jit_solution(3873085965169618669)
XLA Ops:
  2.9 4.1 multiply_reduce_fusion.2
  7.7 41.7 %multiply_convert_fusion.2 = bf16[4096,4096]{1,0:T(8,128)(2,1)} fusion(bf16[4096,768]{1,0:T(8,128)(2,1)} %param.8, f32[]{:T(128)} %bitcast.5, f32[4096]{0:T(1024)S(1)} %multiply_reduce_fusion.2, f32[]{:T(128)} %bitcast.38), kind=kOutput, calls=%fused_computation.12 | convolution fusion | flops 25904021504 | bytes 39862280 | tf_op jit(solution)/shard_map/if,jf->ij/dot_general | solution.py:12
  49.4 15.0 %fusion.8 = f32[4096,128]{1,0:T(8,128)S(1)} fusion(bf16[4096,4096]{1,0:T(8,128)(2,1)} %multiply_convert_fusion.2, bf16[4096,128]{1,0:T(8,128)(2,1)} %copy.33), kind=kOutput, calls=%fused_computation.14 | convolution fusion | flops 4294967296 | bytes 36700160 | tf_op jit(solution)/shard_map/dot_general | solution.py:15
  64.4 5.8 copy.6
  70.2 439.4 %while.32 = (s32[]{:T(128)}, bf16[4096,768]{1,0:T(8,128)(2,1)}, bf16[4096,128]{1,0:T(8,128)(2,1)}, f32[4096,128]{1,0:T(8,128)S(1)}, f32[1]{0:T(128)}, /*index=5*...) while((s32[]{:T(128)}, bf16[4096,768]{1,0:T(8,128)(2,1)}, bf16[4096,128]{1,0:T(8,128)(2,1)}, ...), condition=%wide.region_3.0_spmd, body=%wide.region_1.0_spmd.sunk | while | flops 30208946176 | bytes 68206768 | solution.py:28
  87.0 79.2 %collective-permute-done.1 = bf16[4096,128]{1,0:T(8,128)(2,1)S(1)} collective-permute-done((bf16[4096,128]{1,0:T(8,128)(2,1)}, bf16[4096,128]{1,0:T(8,128)(2,1)S(1)}, u32[]{:S(2)}, u32[]{:S(2)}) %collective-permute-start.1) | collective-permute-done | bytes 1048608 | tf_op jit(solution)/shard_map/while/body/eval_jaxpr/ppermute | solution.py:23
  167.2 4.1 multiply_reduce_fusion.5
  171.3 5.8 copy.14
  177.1 49.1 %fusion.33 = f32[4096,128]{1,0:T(8,128)S(1)} fusion(f32[4096,128]{1,0:T(8,128)S(1)} %get-tuple-element.339, bf16[4096,128]{1,0:T(8,128)(2,1)S(1)} %collective-permute-done.1, bf16[4096,768]{1,0:T(8,128)(2,1)} %get-tuple-element.351, bf16[4096,768]{1,0:T(8,128)(2,1)} %collective-permute-done, f32[]{:T(128)} %bitcast.31, ...), kind=kOutput, calls=%fused_computation.3.clone.1 | convolution fusion | flops 30199513088 | bytes 17858568 | tf_op jit(solution)/shard_map/while/body/eval_jaxpr/dot_general | solution.py:15
  228.7 79.2 %collective-permute-done.1 = bf16[4096,128]{1,0:T(8,128)(2,1)S(1)} collective-permute-done((bf16[4096,128]{1,0:T(8,128)(2,1)}, bf16[4096,128]{1,0:T(8,128)(2,1)S(1)}, u32[]{:S(2)}, u32[]{:S(2)}) %collective-permute-start.1) | collective-permute-done | bytes 1048608 | tf_op jit(solution)/shard_map/while/body/eval_jaxpr/ppermute | solution.py:23
  308.9 4.1 multiply_reduce_fusion.5
  313.0 5.8 copy.14
  318.8 49.1 %fusion.33 = f32[4096,128]{1,0:T(8,128)S(1)} fusion(f32[4096,128]{1,0:T(8,128)S(1)} %get-tuple-element.339, bf16[4096,128]{1,0:T(8,128)(2,1)S(1)} %collective-permute-done.1, bf16[4096,768]{1,0:T(8,128)(2,1)} %get-tuple-element.351, bf16[4096,768]{1,0:T(8,128)(2,1)} %collective-permute-done, f32[]{:T(128)} %bitcast.31, ...), kind=kOutput, calls=%fused_computation.3.clone.1 | convolution fusion | flops 30199513088 | bytes 17858568 | tf_op jit(solution)/shard_map/while/body/eval_jaxpr/dot_general | solution.py:15
  370.4 79.2 %collective-permute-done.1 = bf16[4096,128]{1,0:T(8,128)(2,1)S(1)} collective-permute-done((bf16[4096,128]{1,0:T(8,128)(2,1)}, bf16[4096,128]{1,0:T(8,128)(2,1)S(1)}, u32[]{:S(2)}, u32[]{:S(2)}) %collective-permute-start.1) | collective-permute-done | bytes 1048608 | tf_op jit(solution)/shard_map/while/body/eval_jaxpr/ppermute | solution.py:23
  450.6 4.1 multiply_reduce_fusion.5
  454.7 5.8 copy.14
  460.4 49.1 %fusion.33 = f32[4096,128]{1,0:T(8,128)S(1)} fusion(f32[4096,128]{1,0:T(8,128)S(1)} %get-tuple-element.339, bf16[4096,128]{1,0:T(8,128)(2,1)S(1)} %collective-permute-done.1, bf16[4096,768]{1,0:T(8,128)(2,1)} %get-tuple-element.351, bf16[4096,768]{1,0:T(8,128)(2,1)} %collective-permute-done, f32[]{:T(128)} %bitcast.31, ...), kind=kOutput, calls=%fused_computation.3.clone.1 | convolution fusion | flops 30199513088 | bytes 17858568 | tf_op jit(solution)/shard_map/while/body/eval_jaxpr/dot_general | solution.py:15
  509.7 16.6 %fusion.9 = f32[4096,128]{1,0:T(8,128)} fusion(bf16[4096,4096]{1,0:T(8,128)(2,1)} %multiply_convert_fusion.2, bf16[4096,128]{1,0:T(8,128)(2,1)S(1)} %convert_element_type.32), kind=kOutput, calls=%fused_computation.15 | convolution fusion | flops 4294967296 | bytes 36700160 | tf_op jit(solution)/shard_map/dot_general | solution.py:15
  526.3 2.7 copy.18
  528.9 423.2 %while.33 = (s32[]{:T(128)}, bf16[4096,768]{1,0:T(8,128)(2,1)}, bf16[4096,128]{1,0:T(8,128)(2,1)S(1)}, f32[4096,128]{1,0:T(8,128)}, f32[1]{0:T(128)}, /*index=5*...) while((s32[]{:T(128)}, bf16[4096,768]{1,0:T(8,128)(2,1)}, ...), condition=%wide.region_6.0_spmd, body=%wide.region_4.0_spmd.sunk | while | flops 30208946176 | bytes 68206768 | solution.py:28
  531.4 79.2 %collective-permute-done.3 = bf16[4096,128]{1,0:T(8,128)(2,1)S(1)} collective-permute-done((bf16[4096,128]{1,0:T(8,128)(2,1)S(1)}, bf16[4096,128]{1,0:T(8,128)(2,1)S(1)}, u32[]{:S(2)}, u32[]{:S(2)}) %collective-permute-start.3) | collective-permute-done | bytes 1048608 | tf_op jit(solution)/shard_map/while/body/eval_jaxpr/ppermute | solution.py:23
  610.7 4.1 multiply_reduce_fusion.6
  614.8 5.9 copy.26
  620.6 49.4 %fusion.37 = f32[4096,128]{1,0:T(8,128)} fusion(f32[4096,128]{1,0:T(8,128)} %get-tuple-element.366, bf16[4096,128]{1,0:T(8,128)(2,1)S(1)} %collective-permute-done.3, bf16[4096,768]{1,0:T(8,128)(2,1)} %get-tuple-element.378, bf16[4096,768]{1,0:T(8,128)(2,1)} %collective-permute-done.2, f32[]{:T(128)} %bitcast.36, ...), kind=kOutput, calls=%fused_computation.9.clone.1 | convolution fusion | flops 30199513088 | bytes 17858568 | tf_op jit(solution)/shard_map/while/body/eval_jaxpr/dot_general | solution.py:15
  672.4 79.2 %collective-permute-done.3 = bf16[4096,128]{1,0:T(8,128)(2,1)S(1)} collective-permute-done((bf16[4096,128]{1,0:T(8,128)(2,1)S(1)}, bf16[4096,128]{1,0:T(8,128)(2,1)S(1)}, u32[]{:S(2)}, u32[]{:S(2)}) %collective-permute-start.3) | collective-permute-done | bytes 1048608 | tf_op jit(solution)/shard_map/while/body/eval_jaxpr/ppermute | solution.py:23
  751.7 4.1 multiply_reduce_fusion.6
  755.8 5.9 copy.26
  761.7 49.4 %fusion.37 = f32[4096,128]{1,0:T(8,128)} fusion(f32[4096,128]{1,0:T(8,128)} %get-tuple-element.366, bf16[4096,128]{1,0:T(8,128)(2,1)S(1)} %collective-permute-done.3, bf16[4096,768]{1,0:T(8,128)(2,1)} %get-tuple-element.378, bf16[4096,768]{1,0:T(8,128)(2,1)} %collective-permute-done.2, f32[]{:T(128)} %bitcast.36, ...), kind=kOutput, calls=%fused_computation.9.clone.1 | convolution fusion | flops 30199513088 | bytes 17858568 | tf_op jit(solution)/shard_map/while/body/eval_jaxpr/dot_general | solution.py:15
  813.5 79.2 %collective-permute-done.3 = bf16[4096,128]{1,0:T(8,128)(2,1)S(1)} collective-permute-done((bf16[4096,128]{1,0:T(8,128)(2,1)S(1)}, bf16[4096,128]{1,0:T(8,128)(2,1)S(1)}, u32[]{:S(2)}, u32[]{:S(2)}) %collective-permute-start.3) | collective-permute-done | bytes 1048608 | tf_op jit(solution)/shard_map/while/body/eval_jaxpr/ppermute | solution.py:23
  892.8 4.1 multiply_reduce_fusion.6
  896.9 5.9 copy.26
  902.7 49.4 %fusion.37 = f32[4096,128]{1,0:T(8,128)} fusion(f32[4096,128]{1,0:T(8,128)} %get-tuple-element.366, bf16[4096,128]{1,0:T(8,128)(2,1)S(1)} %collective-permute-done.3, bf16[4096,768]{1,0:T(8,128)(2,1)} %get-tuple-element.378, bf16[4096,768]{1,0:T(8,128)(2,1)} %collective-permute-done.2, f32[]{:T(128)} %bitcast.36, ...), kind=kOutput, calls=%fused_computation.9.clone.1 | convolution fusion | flops 30199513088 | bytes 17858568 | tf_op jit(solution)/shard_map/while/body/eval_jaxpr/dot_general | solution.py:15
  (31 shorter events, 21.2 us)
Async XLA Ops:
  83.6 83.6 %collective-permute-start = (bf16[4096,768]{1,0:T(8,128)(2,1)}, bf16[4096,768]{1,0:T(8,128)(2,1)}, u32[]{:S(2)}, u32[]{:S(2)}) collective-permute-start(bf16[4096,768]{1,0:T(8,128)(2,1)} %get-tuple-element.337), channel_id=1, source_target_pairs={{0,1},{1,2},{2,3},{3,0},{4,5},{5,6},{6,7},{7,4},{8,9},{9,10},{10,1... | collective-permute-start | bytes 18874376 | tf_op jit(solution)/shard_map/while/body/eval_jaxpr/ppermute | solution.py:22
  84.4 81.8 %collective-permute-start.1 = (bf16[4096,128]{1,0:T(8,128)(2,1)}, bf16[4096,128]{1,0:T(8,128)(2,1)S(1)}, u32[]{:S(2)}, u32[]{:S(2)}) collective-permute-start(bf16[4096,128]{1,0:T(8,128)(2,1)} %get-tuple-element.338), channel_id=1, source_target_pairs={{0,1},{1,2},{2,3},{3,0},{4,5},{5,6},{6,7},{7,4},{8,9},{9,10},{10,1... | collective-permute-start | bytes 3145736 | tf_op jit(solution)/shard_map/while/body/eval_jaxpr/ppermute | solution.py:23
  226.2 82.7 %collective-permute-start = (bf16[4096,768]{1,0:T(8,128)(2,1)}, bf16[4096,768]{1,0:T(8,128)(2,1)}, u32[]{:S(2)}, u32[]{:S(2)}) collective-permute-start(bf16[4096,768]{1,0:T(8,128)(2,1)} %get-tuple-element.337), channel_id=1, source_target_pairs={{0,1},{1,2},{2,3},{3,0},{4,5},{5,6},{6,7},{7,4},{8,9},{9,10},{10,1... | collective-permute-start | bytes 18874376 | tf_op jit(solution)/shard_map/while/body/eval_jaxpr/ppermute | solution.py:22
  226.3 81.6 %collective-permute-start.1 = (bf16[4096,128]{1,0:T(8,128)(2,1)}, bf16[4096,128]{1,0:T(8,128)(2,1)S(1)}, u32[]{:S(2)}, u32[]{:S(2)}) collective-permute-start(bf16[4096,128]{1,0:T(8,128)(2,1)} %get-tuple-element.338), channel_id=1, source_target_pairs={{0,1},{1,2},{2,3},{3,0},{4,5},{5,6},{6,7},{7,4},{8,9},{9,10},{10,1... | collective-permute-start | bytes 3145736 | tf_op jit(solution)/shard_map/while/body/eval_jaxpr/ppermute | solution.py:23
  367.9 82.7 %collective-permute-start = (bf16[4096,768]{1,0:T(8,128)(2,1)}, bf16[4096,768]{1,0:T(8,128)(2,1)}, u32[]{:S(2)}, u32[]{:S(2)}) collective-permute-start(bf16[4096,768]{1,0:T(8,128)(2,1)} %get-tuple-element.337), channel_id=1, source_target_pairs={{0,1},{1,2},{2,3},{3,0},{4,5},{5,6},{6,7},{7,4},{8,9},{9,10},{10,1... | collective-permute-start | bytes 18874376 | tf_op jit(solution)/shard_map/while/body/eval_jaxpr/ppermute | solution.py:22
  368.0 81.6 %collective-permute-start.1 = (bf16[4096,128]{1,0:T(8,128)(2,1)}, bf16[4096,128]{1,0:T(8,128)(2,1)S(1)}, u32[]{:S(2)}, u32[]{:S(2)}) collective-permute-start(bf16[4096,128]{1,0:T(8,128)(2,1)} %get-tuple-element.338), channel_id=1, source_target_pairs={{0,1},{1,2},{2,3},{3,0},{4,5},{5,6},{6,7},{7,4},{8,9},{9,10},{10,1... | collective-permute-start | bytes 3145736 | tf_op jit(solution)/shard_map/while/body/eval_jaxpr/ppermute | solution.py:23
  509.6 16.7 %slice-start = ((s8[6291456]{0:T(1024)(128)(4,1)}), s8[4194304]{0:T(1024)(128)(4,1)S(1)}, s32[]{:S(2)}) async-start(s8[6291456]{0:T(1024)(128)(4,1)} %bitcast.39), calls=%async_computation | async-start | bytes 8388608
  509.7 16.6 %slice-start.1 = ((s8[6291456]{0:T(1024)(128)(4,1)}), s8[2097152]{0:T(1024)(128)(4,1)S(1)}, s32[]{:S(2)}) async-start(s8[6291456]{0:T(1024)(128)(4,1)} %bitcast.39), calls=%async_computation.1 | async-start | bytes 4194304
  528.9 81.7 %collective-permute-start.2 = (bf16[4096,768]{1,0:T(8,128)(2,1)}, bf16[4096,768]{1,0:T(8,128)(2,1)}, u32[]{:S(2)}, u32[]{:S(2)}) collective-permute-start(bf16[4096,768]{1,0:T(8,128)(2,1)} %get-tuple-element.364), channel_id=1, source_target_pairs={{0,1},{1,2},{2,3},{3,0},{4,5},{5,6},{6,7},{7,4},{8,9},{9,10},{10,1... | collective-permute-start | bytes 18874376 | tf_op jit(solution)/shard_map/while/body/eval_jaxpr/ppermute | solution.py:22
  528.9 81.6 %collective-permute-start.3 = (bf16[4096,128]{1,0:T(8,128)(2,1)S(1)}, bf16[4096,128]{1,0:T(8,128)(2,1)S(1)}, u32[]{:S(2)}, u32[]{:S(2)}) collective-permute-start(bf16[4096,128]{1,0:T(8,128)(2,1)S(1)} %get-tuple-element.365), channel_id=1, source_target_pairs={{0,1},{1,2},{2,3},{3,0},{4,5},{5,6},{6,7},{7,4},{8,9},{9,10},{10,1... | collective-permute-start | bytes 3145736 | tf_op jit(solution)/shard_map/while/body/eval_jaxpr/ppermute | solution.py:23
  670.0 81.7 %collective-permute-start.2 = (bf16[4096,768]{1,0:T(8,128)(2,1)}, bf16[4096,768]{1,0:T(8,128)(2,1)}, u32[]{:S(2)}, u32[]{:S(2)}) collective-permute-start(bf16[4096,768]{1,0:T(8,128)(2,1)} %get-tuple-element.364), channel_id=1, source_target_pairs={{0,1},{1,2},{2,3},{3,0},{4,5},{5,6},{6,7},{7,4},{8,9},{9,10},{10,1... | collective-permute-start | bytes 18874376 | tf_op jit(solution)/shard_map/while/body/eval_jaxpr/ppermute | solution.py:22
  670.0 81.6 %collective-permute-start.3 = (bf16[4096,128]{1,0:T(8,128)(2,1)S(1)}, bf16[4096,128]{1,0:T(8,128)(2,1)S(1)}, u32[]{:S(2)}, u32[]{:S(2)}) collective-permute-start(bf16[4096,128]{1,0:T(8,128)(2,1)S(1)} %get-tuple-element.365), channel_id=1, source_target_pairs={{0,1},{1,2},{2,3},{3,0},{4,5},{5,6},{6,7},{7,4},{8,9},{9,10},{10,1... | collective-permute-start | bytes 3145736 | tf_op jit(solution)/shard_map/while/body/eval_jaxpr/ppermute | solution.py:23
  811.1 81.7 %collective-permute-start.2 = (bf16[4096,768]{1,0:T(8,128)(2,1)}, bf16[4096,768]{1,0:T(8,128)(2,1)}, u32[]{:S(2)}, u32[]{:S(2)}) collective-permute-start(bf16[4096,768]{1,0:T(8,128)(2,1)} %get-tuple-element.364), channel_id=1, source_target_pairs={{0,1},{1,2},{2,3},{3,0},{4,5},{5,6},{6,7},{7,4},{8,9},{9,10},{10,1... | collective-permute-start | bytes 18874376 | tf_op jit(solution)/shard_map/while/body/eval_jaxpr/ppermute | solution.py:22
  811.1 81.6 %collective-permute-start.3 = (bf16[4096,128]{1,0:T(8,128)(2,1)S(1)}, bf16[4096,128]{1,0:T(8,128)(2,1)S(1)}, u32[]{:S(2)}, u32[]{:S(2)}) collective-permute-start(bf16[4096,128]{1,0:T(8,128)(2,1)S(1)} %get-tuple-element.365), channel_id=1, source_target_pairs={{0,1},{1,2},{2,3},{3,0},{4,5},{5,6},{6,7},{7,4},{8,9},{9,10},{10,1... | collective-permute-start | bytes 3145736 | tf_op jit(solution)/shard_map/while/body/eval_jaxpr/ppermute | solution.py:23
where the time goes:
time: 960 us; the launch traced here: 953 us
  waiting for transfers between devices  475 us (49%)
  matrix products  369 us (38%)
  local copies, waits for them, and re-layouts  48.8 us (5%)
  other arithmetic  28.7 us (3%)
  starting transfers between devices  15.6 us (2%)
  loops' own time  13.6 us (1%)
    ppermute x6, waiting for transfers between devices, visit_step(): v_vis = lax.ppermute(v_vis, 'row', shift_pairs)  475 us
    dot_general x8, matrix products, kernel_product(): return jnp.dot(kern_tile, v_cols, preferred_element_type=jnp.float32)  327 us
    dot_general x1, matrix products, kernel_product(): jnp.einsum('if,jf->ij', x_rows, x_cols, preferred_element_type=jnp.float32)  41.7 us
    while x12, local copies, waits for them, and re-layouts  38.1 us
    reduce_sum x6, other arithmetic, visit_step(): norm_vis = jnp.sum(jnp.square(x_vis.astype(jnp.float32)), axis=1)  24.5 us
  transfers between devices with their start and end apart: 12, of which 6 were waited for; matrix products, arithmetic and copies ran while one was open for 0% of the time, Pallas kernels for 0%

commit v1 on v0

v1 whole, which is shorter than its diff:
```python
import functools

import jax
import jax.numpy as jnp
from jax import lax
from jax.experimental import pallas as pl
from jax.experimental.pallas import tpu as pltpu
from jax.sharding import PartitionSpec as P

MESH = pl.DeviceIdType.MESH
F32 = jnp.float32
BF16 = jnp.bfloat16
LOG2E = 1.4426950408889634

ROWS = 4096
FEAT = 768
COLS = 128
CH = 512
NB = ROWS // CH
NQ = 4 * NB
TI = 256
NT = ROWS // TI
NS = 7
NSTREAM = 3
NKEEP = NS - NSTREAM
NH = NQ - NKEEP


def body(x_ref, v_ref, ell_ref, s_ref, w_ref, k_hbm, xp_hbm,
         xbuf, xt, vg, yg, vt, hj, hi, acc, slots,
         px_s, px_r, pv_s, pv_r, x_s, x_r, v_s, v_r, fx_s, fx_r, fv_s, fv_r,
         yp_s, yp_r, yx_s, yx_r, yf_s, yf_r, st_sem, vl_sem, ko_sem, kl_sem):
    task = lax.axis_index("task")
    me = lax.axis_index("row")
    partner = me + 1 - 2 * lax.rem(me, 2)
    peer = lax.rem(me + 2, 4)

    barrier = pltpu.get_barrier_semaphore()
    for dev in (partner, peer):
        pl.semaphore_signal(barrier, inc=1, device_id=(task, dev), device_id_type=MESH)
    pl.semaphore_wait(barrier, 2)

    def remote(src, dst, send, recv, dev):
        return pltpu.make_async_remote_copy(
            src_ref=src, dst_ref=dst, send_sem=send, recv_sem=recv,
            device_id=(task, dev), device_id_type=MESH)

    def x_cross(k):
        return remote(x_ref.at[k], xbuf.at[2 + 2 * k], x_s.at[k], x_r.at[k], peer)

    def v_cross(k):
        return remote(v_ref.at[k], vg.at[16 + 2 * k], v_s.at[k], v_r.at[k], peer)

    def x_fwd(k):
        return remote(xbuf.at[2 + 2 * k], xbuf.at[3 + 2 * k], fx_s.at[k], fx_r.at[k], partner)

    def v_fwd(k):
        return remote(vg.at[16 + 2 * k], vg.at[17 + 2 * k], fv_s.at[k], fv_r.at[k], partner)

    x_part = remote(x_ref, xp_hbm, px_s, px_r, partner)
    v_part = remote(v_ref, vg.at[pl.ds(NB, NB)], pv_s, pv_r, partner)

    def y_part(k):
        return remote(yg.at[k], yg.at[NB + k], yp_s.at[k], yp_r.at[k], partner)

    def y_cross(k):
        return remote(yg.at[k], yg.at[16 + 2 * k], yx_s.at[k], yx_r.at[k], peer)

    def y_fwd(k):
        return remote(yg.at[16 + 2 * k], yg.at[17 + 2 * k], yf_s.at[k], yf_r.at[k], partner)

    def stage_own(k, buf):
        return pltpu.make_async_copy(x_ref.at[k], xbuf.at[buf], st_sem.at[buf])

    def stage_part(k, buf):
        return pltpu.make_async_copy(xp_hbm.at[k], xbuf.at[buf], st_sem.at[buf])

    def k_out(q, slot):
        return pltpu.make_async_copy(slots.at[slot], k_hbm.at[q], ko_sem.at[slot])

    def k_load(q, slot):
        return pltpu.make_async_copy(k_hbm.at[q], slots.at[slot], kl_sem.at[slot])

    v_own = pltpu.make_async_copy(v_ref, vg.at[pl.ds(0, NB)], vl_sem)

    stage_own(0, 0).start()

    @pl.loop(0, NB)
    def _(k):
        v_cross(k).start()
        x_cross(k).start()

    v_part.start()
    x_part.start()
    v_own.start()

    @pl.loop(0, NB)
    def _(k):
        buf = lax.rem(k, 2)

        @pl.when(k + 1 < NB)
        def _():
            stage_own(k + 1, 1 - buf).start()

        stage_own(k, buf).wait()
        xc = xbuf[buf]
        cols = pl.ds(pl.multiple_of(k * CH, CH), CH)
        xct = xc.T
        xt[:, cols] = xct
        hi[:, cols] = 0.5 * jnp.sum(jnp.square(xct.astype(F32)), axis=0, keepdims=True)

    stage_own(0, 0).start()
    acc[...] = jnp.zeros_like(acc)
    v_own.wait()

    ell = ell_ref[0]
    s = s_ref[0]
    ratio = jnp.full((8, 128), -2.0 * LOG2E, F32) / jnp.full((8, 128), 2.0 * ell * ell, F32)
    scale_e = ratio[0:1, :]

    @pl.loop(0, NQ)
    def _(q):
        k = lax.div(q - 16, 2)
        slot = lax.rem(q, NS)

        @pl.when(jnp.logical_and(q >= 1, q - 1 < NH))
        def _():
            k_out(q - 1, lax.rem(q - 1 + NS, NS)).start()

        @pl.when(q >= NS)
        def _():
            k_out(q - NS, slot).wait()

        @pl.when(q == 7)
        def _():
            x_part.wait_recv()
            v_part.wait_recv()

        @pl.when(q < 7)
        def _():
            stage_own(q + 1, lax.rem(q + 1, 2)).start()

        @pl.when(jnp.logical_and(q >= 7, q < 15))
        def _():
            stage_part(q - 7, lax.rem(q + 1, 2)).start()

        @pl.when(q < 16)
        def _():
            stage_own(0, lax.rem(q, 2)).wait()

        @pl.when(jnp.logical_and(q >= 16, lax.rem(q, 2) == 0))
        def _():
            x_cross(k).wait_recv()
            x_fwd(k).start()
            v_cross(k).wait_recv()
            v_fwd(k).start()

        @pl.when(jnp.logical_and(q >= 16, lax.rem(q, 2) == 1))
        def _():
            x_fwd(k).wait_recv()
            v_fwd(k).wait_recv()

        xi = jnp.where(q < 16, lax.rem(q, 2), q - 14)
        xc_ref = xbuf.at[xi]
        vt[...] = vg[q].T
        hj[...] = jnp.broadcast_to(
            0.5 * jnp.sum(jnp.square(xc_ref[...].astype(F32)), axis=1, keepdims=True), (CH, 128))

        def gen(t):
            cols = pl.ds(t * TI, TI)
            g = jnp.dot(xc_ref[...], xt[:, cols], preferred_element_type=F32)
            h = jnp.concatenate([hj[...]] * (TI // 128), axis=1)
            c = jnp.concatenate([scale_e] * (TI // 128), axis=1)
            d = jnp.maximum(h + hi[:, cols] - g, 0.0)
            slots[slot, :, cols] = (s * jnp.exp2(d * c)).astype(BF16)

        def app(t):
            cols = pl.ds(t * TI, TI)
            acc[:, cols] += jnp.dot(vt[...], slots[slot, :, cols], preferred_element_type=F32)

        for t in range(NT + 2):
            if t < NT:
                gen(t)
            if t >= 2:
                app(t - 2)

    for k in range(NB + 1):
        if k < NB:
            yg[k] = acc[:, k * CH:(k + 1) * CH].astype(BF16)
        if k >= 1:
            y_cross(k - 1).start()
            y_part(k - 1).start()
    acc[...] = jnp.zeros_like(acc)

    @pl.loop(0, NSTREAM)
    def _(i):
        k_out(NH - NSTREAM + i, NKEEP + i).wait()
        k_load(i, NKEEP + i).start()

    @pl.loop(0, NQ)
    def _(q):
        k = lax.div(q - 16, 2)
        slot = jnp.where(q < NH, NKEEP + lax.rem(q, NSTREAM), q - NH)

        @pl.when(jnp.logical_and(q >= NB, q < 16))
        def _():
            y_part(q - NB).wait_recv()

        @pl.when(q == 16)
        def _():
            y_cross(0).wait_recv()
            y_fwd(0).start()

        @pl.when(jnp.logical_and(jnp.logical_and(q >= 16, lax.rem(q, 2) == 0), k + 1 < NB))
        def _():
            y_cross(k + 1).wait_recv()
            y_fwd(k + 1).start()

        @pl.when(jnp.logical_and(q >= 16, lax.rem(q, 2) == 1))
        def _():
            y_fwd(k).wait_recv()

        @pl.when(q < NH)
        def _():
            k_load(q, slot).wait()

        for t in range(ROWS // 512):
            cols = pl.ds(t * 512, 512)
            acc[:, cols] += jnp.dot(yg[q], slots[slot, :, cols], preferred_element_type=F32)

        @pl.when(q + NSTREAM < NH)
        def _():
            k_load(q + NSTREAM, slot).start()

    for t in range(ROWS // 512):
        w_ref[t * 512:(t + 1) * 512, :] = acc[:, t * 512:(t + 1) * 512].T

    x_part.wait_send()
    v_part.wait_send()

    @pl.loop(0, NB)
    def _(k):
        x_cross(k).wait_send()
        v_cross(k).wait_send()
        x_fwd(k).wait_send()
        v_fwd(k).wait_send()
        y_part(k).wait_send()
        y_cross(k).wait_send()
        y_fwd(k).wait_send()


def solution(mesh):
    def local_program(x_loc, v_loc, length_scale, out_scale):
        dma = pltpu.SemaphoreType.DMA
        any_spec = pl.BlockSpec(memory_space=pl.ANY)
        smem = pl.BlockSpec(memory_space=pltpu.SMEM)
        out = pl.pallas_call(
            body,
            out_shape=[
                jax.ShapeDtypeStruct((ROWS, COLS), F32),
                jax.ShapeDtypeStruct((NH, CH, ROWS), BF16),
                jax.ShapeDtypeStruct((NB, CH, FEAT), BF16),
            ],
            in_specs=[any_spec, any_spec, smem, smem],
            out_specs=[pl.BlockSpec(memory_space=pltpu.VMEM), any_spec, any_spec],
            scratch_shapes=[
                pltpu.VMEM((2 + 2 * NB, CH, FEAT), BF16),
                pltpu.VMEM((FEAT, ROWS), BF16),
                pltpu.VMEM((NQ, CH, COLS), BF16),
                pltpu.VMEM((NQ, COLS, CH), BF16),
                pltpu.VMEM((COLS, CH), BF16),
                pltpu.VMEM((CH, 128), F32),
                pltpu.VMEM((1, ROWS), F32),
                pltpu.VMEM((COLS, ROWS), F32),
                pltpu.VMEM((NS, CH, ROWS), BF16),
                dma, dma, dma, dma,
                dma((NB,)), dma((NB,)), dma((NB,)), dma((NB,)),
                dma((NB,)), dma((NB,)), dma((NB,)), dma((NB,)),
                dma((NB,)), dma((NB,)), dma((NB,)), dma((NB,)), dma((NB,)), dma((NB,)),
                dma((2,)), dma, dma((NS,)), dma((NS,)),
            ],
            compiler_params=pltpu.CompilerParams(
                collective_id=0, has_side_effects=True, vmem_limit_bytes=67043328),
            name="two_products",
        )(x_loc.reshape(NB, CH, FEAT), v_loc.reshape(NB, CH, COLS), length_scale, out_scale)
        return out[0]

    row_spec = P(("task", "row"), None)
    return jax.shard_map(local_program, mesh=mesh, in_specs=(row_spec, row_spec, P("task"), P("task")),
                         out_specs=row_spec, check_vma=False)
```

time: 960 us -> 218 us (0.23)
  waiting for transfers between devices: 475 us -> 0 us
  matrix products: 369 us -> 0 us
  Pallas kernels: 0 us -> 213 us
  local copies, waits for them, and re-layouts: 48.8 us -> 3.05 us
  other arithmetic: 28.7 us -> 0 us
  starting transfers between devices: 15.6 us -> 0 us
  loops' own time: 13.6 us -> 0 us
    ppermute x12 -> x0, waiting for transfers between devices: 475 us -> none  [the longest x6 475 us: visit_step(): v_vis = lax.ppermute(v_vis, 'row', shift_pairs)]
    dot_general x9 -> x0, matrix products: 369 us -> none  [the longest x8 327 us: kernel_product(): return jnp.dot(kern_tile, v_cols, preferred_element_type=jnp.float32)]
    pallas_call x0 -> x1, Pallas kernels: none -> 213 us  [local_program(): pl.pallas_call(body, out_shape=[jax.ShapeDtypeStruct((ROWS, COLS), F32),...]
    while x12 -> x0, local copies, waits for them, and re-layouts: 38.1 us -> none
    reduce_sum x7 -> x0, other arithmetic: 28.6 us -> none  [the longest x6 24.5 us: visit_step(): norm_vis = jnp.sum(jnp.square(x_vis.astype(jnp.float32)), axis=1)]
    ppermute x12 -> x0, starting transfers between devices: 15.6 us -> none  [the longest x6 14.7 us: visit_step(): v_vis = lax.ppermute(v_vis, 'row', shift_pairs)]
    another operation x2 -> x0, loops' own time: 13.6 us -> none  [kernel_pass(): final_state = lax.fori_loop(1, n_row, visit_step, (x_loc, v_loc, own_part))]
  transfers between devices with their start and end apart: 12 -> 0, of which waited for: 6 -> 0; matrix products, arithmetic and copies ran while one was open for 0% -> 0% of each run, Pallas kernels for 0% -> 0%
where the time goes in v1:
time: 218 us
  Pallas kernels  213 us (98%)
  local copies, waits for them, and re-layouts  3.05 us (1%)
    pallas_call x1, Pallas kernels, local_program(): pl.pallas_call(body, out_shape=[jax.ShapeDtypeStruct((ROWS, COLS), F32),...  213 us

profile of v1, /device:TPU:0, one launch (start us, length us, event | category | flops | bytes accessed | tf_op | source)
XLA Modules:
  0.0 217.8 jit_solution(12247643211275983252)
XLA Ops:
  1.3 213.5 %two_products.1 = (f32[4096,128]{1,0:T(8,128)}, bf16[28,512,4096]{2,1,0:T(8,128)(2,1)}, bf16[8,512,768]{2,1,0:T(8,128)(2,1)}) custom-call(bf16[8,512,768]{2,1,0:T(8,128)(2,1)} %bitcast.2, bf16[8,512,128]{2,1,0:T(8,128)(2,1)} %bitcast.3, f32[1]{0:T(128)S(6)} %copy.6.ell_ref, f32[1]{0:T(128)S(6)} %copy.7.s_ref), custom_call_target="tpu_custom_call" | custom-call | tf_op jit(solution)/shard_map/two_products/pallas_call | solution.py:257
  214.8 3.0 %copy.8 = f32[4096,128]{1,0:T(8,128)} copy(f32[4096,128]{1,0:T(8,128)} %get-tuple-element.6) | data formatting | bytes 4194304

commit v2 on v1

v2 whole, which is shorter than its diff:
```python
import jax
import jax.numpy as jnp
from jax import lax
from jax.experimental import pallas as pl
from jax.experimental.pallas import tpu as pltpu
from jax.sharding import PartitionSpec as P

MESH = pl.DeviceIdType.MESH
F32 = jnp.float32
BF16 = jnp.bfloat16
LOG2E = 1.4426950408889634

ROWS = 4096
FEAT = 768
COLS = 128
CH = 512
NB = ROWS // CH
NQ = 4 * NB
NM = NQ - 1
NL = NQ - 2
TI = 256
NT = ROWS // TI
HALF = CH // 2
NS = 11
NSTREAM = 3
NH = NQ - (NS - NSTREAM)


def body(x_ref, v_ref, ell_ref, s_ref, w_ref, k_hbm, xg, vg,
         xbuf, vbuf, xt, yg, vt, hj, hi, acc, wacc, slots,
         px_s, px_r, pv_s, pv_r, x_s, x_r, v_s, v_r, fx_s, fx_r, fv_s, fv_r,
         yp_s, yp_r, yx_s, yx_r, yf_s, yf_r, st_sem, sv_sem, ko_sem, kl_sem):
    task = lax.axis_index("task")
    me = lax.axis_index("row")
    partner = me + 1 - 2 * lax.rem(me, 2)
    peer = lax.rem(me + 2, 4)

    barrier = pltpu.get_barrier_semaphore()
    for dev in (peer, partner):
        pl.semaphore_signal(barrier, inc=1, device_id=(task, dev), device_id_type=MESH)
    pl.semaphore_wait(barrier, 2)

    def remote(src, dst, send, recv, dev):
        return pltpu.make_async_remote_copy(
            src_ref=src, dst_ref=dst, send_sem=send, recv_sem=recv,
            device_id=(task, dev), device_id_type=MESH)

    def x_cross(k):
        return remote(x_ref.at[k], xg.at[8 + 2 * k], x_s.at[k], x_r.at[k], peer)

    def v_cross(k):
        return remote(v_ref.at[k], vg.at[8 + 2 * k], v_s.at[k], v_r.at[k], peer)

    def x_fwd(k):
        return remote(xg.at[8 + 2 * k], xg.at[9 + 2 * k], fx_s.at[k], fx_r.at[k], partner)

    def v_fwd(k):
        return remote(vg.at[8 + 2 * k], vg.at[9 + 2 * k], fv_s.at[k], fv_r.at[k], partner)

    last = NB - 1
    def halves(r, i):
        return r.at[pl.ds(i * HALF, HALF)]

    x_last = [remote(halves(x_ref.at[last], i), halves(xbuf.at[2 + i], 0), x_s.at[last + i], x_r.at[last + i], peer)
              for i in range(2)]
    v_last = [remote(halves(v_ref.at[last], i), halves(vbuf.at[2 + i], 0), v_s.at[last + i], v_r.at[last + i], peer)
              for i in range(2)]
    x_last_fwd = [remote(halves(xbuf.at[2 + i], 0), halves(xbuf.at[2 + i], 1),
                         fx_s.at[last + i], fx_r.at[last + i], partner) for i in range(2)]
    v_last_fwd = [remote(halves(vbuf.at[2 + i], 0), halves(vbuf.at[2 + i], 1),
                         fv_s.at[last + i], fv_r.at[last + i], partner) for i in range(2)]

    def receive_last(i):
        v_last[i].wait_recv()
        v_last_fwd[i].start()
        x_last[i].wait_recv()
        x_last_fwd[i].start()
        v_last_fwd[i].wait_recv()
        x_last_fwd[i].wait_recv()

    x_part = remote(x_ref, xg.at[pl.ds(0, NB)], px_s, px_r, partner)
    v_part = remote(v_ref, vg.at[pl.ds(0, NB)], pv_s, pv_r, partner)

    def y_part(k):
        return remote(yg.at[k], yg.at[NB + k], yp_s.at[k], yp_r.at[k], partner)

    def y_cross(k):
        return remote(yg.at[k], yg.at[16 + 2 * k], yx_s.at[k], yx_r.at[k], peer)

    def y_fwd(k):
        return remote(yg.at[16 + 2 * k], yg.at[17 + 2 * k], yf_s.at[k], yf_r.at[k], partner)

    def y_piece(k, i):
        return yg.at[k, :, pl.ds(i * HALF, HALF)]

    y_last = [remote(y_piece(last, i), y_piece(NL + i, 0), yx_s.at[last + i], yx_r.at[last + i], peer)
              for i in range(2)]
    y_last_fwd = [remote(y_piece(NL + i, 0), y_piece(NL + i, 1), yf_s.at[last + i], yf_r.at[last + i], partner)
                  for i in range(2)]

    class Stage:
        def __init__(self, x_src, v_src, buf):
            self.x = pltpu.make_async_copy(x_src, xbuf.at[buf], st_sem.at[buf])
            self.v = pltpu.make_async_copy(v_src, vbuf.at[buf], sv_sem.at[buf])

        def start(self):
            self.x.start()
            self.v.start()

        def wait(self):
            self.x.wait()
            self.v.wait()

    def stage_own(q):
        return Stage(x_ref.at[q], v_ref.at[q], lax.rem(q, 2))

    def stage_got(q):
        return Stage(xg.at[q - NB], vg.at[q - NB], lax.rem(q, 2))

    def k_out(q):
        slot = lax.rem(q, NS)
        return pltpu.make_async_copy(slots.at[slot], k_hbm.at[q], ko_sem.at[slot])

    def stream_slot(q):
        return lax.rem(NH - NSTREAM + lax.rem(q, NSTREAM), NS)

    def k_load(q):
        slot = stream_slot(q)
        return pltpu.make_async_copy(k_hbm.at[q], slots.at[slot], kl_sem.at[slot])

    stage_own(0).start()

    @pl.loop(0, last)
    def _(k):
        v_cross(k).start()
        x_cross(k).start()

    for v, x in zip(v_last, x_last):
        v.start()
        x.start()
    v_part.start()
    x_part.start()

    @pl.loop(0, NB)
    def _(k):
        @pl.when(k + 1 < NB)
        def _():
            stage_own(k + 1).start()

        stage_own(k).wait()
        xct = xbuf[lax.rem(k, 2)].T
        cols = pl.ds(pl.multiple_of(k * CH, CH), CH)
        xt[:, cols] = xct
        hi[:, cols] = 0.5 * jnp.sum(jnp.square(xct.astype(F32)), axis=0, keepdims=True)

    stage_own(0).start()
    acc[...] = jnp.zeros_like(acc)
    wacc[...] = jnp.zeros_like(wacc)

    ell = ell_ref[0]
    s = s_ref[0]
    ratio = jnp.full((8, 128), -2.0 * LOG2E, F32) / jnp.full((8, 128), 2.0 * ell * ell, F32)
    scale_e = ratio[0:1, :]

    def prepare(x_i, h_i):
        vt[h_i] = vbuf[x_i].T
        hj[h_i] = jnp.broadcast_to(
            0.5 * jnp.sum(jnp.square(xbuf[x_i].astype(F32)), axis=1, keepdims=True), (CH, 128))

    def gen(x_i, h_i, slot, cols, width):
        g = jnp.dot(xbuf[x_i], xt[:, cols], preferred_element_type=F32)
        h = jnp.concatenate([hj[h_i]] * (width // 128), axis=1)
        c = jnp.concatenate([scale_e] * (width // 128), axis=1)
        d = jnp.maximum(h + hi[:, cols] - g, 0.0)
        slots[slot, :, cols] = (s * jnp.exp2(d * c)).astype(BF16)

    @pl.loop(0, NM)
    def _(q):
        slot = lax.rem(q, NS)
        n = q + 1
        k = lax.div(n - 16, 2)

        @pl.when(jnp.logical_and(q >= 1, q - 1 < NH))
        def _():
            k_out(q - 1).start()

        @pl.when(q >= NS)
        def _():
            k_out(q - NS).wait()

        @pl.when(q >= NM - NSTREAM)
        def _():
            i = q - (NM - NSTREAM)
            k_out(NH - NSTREAM + i).wait()
            k_load(i).start()

        @pl.when(n < NB)
        def _():
            stage_own(n).start()

        @pl.when(n == NB)
        def _():
            x_part.wait_recv()
            v_part.wait_recv()

        @pl.when(jnp.logical_and(n >= 16, n < NL))
        def _():
            @pl.when(lax.rem(n, 2) == 0)
            def _():
                v_cross(k).wait_recv()
                v_fwd(k).start()
                x_cross(k).wait_recv()
                x_fwd(k).start()

            @pl.when(lax.rem(n, 2) == 1)
            def _():
                v_fwd(k).wait_recv()
                x_fwd(k).wait_recv()

        @pl.when(jnp.logical_and(n >= NB, n < NL))
        def _():
            stage_got(n).start()

        @pl.when(q < NL)
        def _():
            stage_own(lax.rem(q, 2)).wait()

        @pl.when(q == NL)
        def _():
            receive_last(0)

        x_i = jnp.where(q < NL, lax.rem(q, 2), 2)
        prepare(x_i, 0)

        def app(t):
            cols = pl.ds(t * TI, TI)
            acc[:, cols] += jnp.dot(vt[0], slots[slot, :, cols], preferred_element_type=F32)

        for t in range(NT + 2):
            if t < NT:
                gen(x_i, 0, slot, pl.ds(t * TI, TI), TI)
            if t >= 2:
                app(t - 2)

    receive_last(1)
    prepare(3, 0)
    slot_b = (NQ - 1) % NS
    k_out(NQ - 1 - NS).wait()

    def second(q, slot):
        for t in range(ROWS // 512):
            cols = pl.ds(t * 512, 512)
            wacc[:, cols] += jnp.dot(yg[q], slots[slot, :, cols], preferred_element_type=F32)

    def second_streamed(q):
        k_load(q).wait()
        second(q, stream_slot(q))

        @pl.when(q + NSTREAM < NH)
        def _():
            k_load(q + NSTREAM).start()

    @pl.loop(0, NB + 1)
    def _(t):
        @pl.when(t < NB)
        def _():
            cols = pl.ds(pl.multiple_of(t * CH, CH), CH)
            gen(3, 0, slot_b, cols, CH)
            y = acc[:, cols] + jnp.dot(vt[0], slots[slot_b, :, cols], preferred_element_type=F32)
            yg[t] = y.astype(BF16)

        @pl.when(t >= 1)
        def _():
            @pl.when(t < NB)
            def _():
                y_cross(t - 1).start()

            @pl.when(t == NB)
            def _():
                y_last[0].start()
                y_last[1].start()

            y_part(t - 1).start()
            second_streamed(t - 1)

    @pl.loop(0, NB)
    def _(i):
        @pl.when(i < last)
        def _():
            y_cross(i).wait_recv()
            y_fwd(i).start()

        @pl.when(i == last)
        def _():
            for c, f in zip(y_last, y_last_fwd):
                c.wait_recv()
                f.start()

        y_part(i).wait_recv()
        second_streamed(NB + i)

    @pl.loop(0, NB)
    def _(i):
        q, r = 16 + i, NH + i
        k = lax.div(i, 2)

        @pl.when(lax.rem(i, 2) == 1)
        def _():
            y_fwd(k).wait_recv()

            @pl.when(k + 4 < last)
            def _():
                y_fwd(k + 4).wait_recv()

        @pl.when(i == 6)
        def _():
            for f in y_last_fwd:
                f.wait_recv()

        k_load(q).wait()
        sq, sr = stream_slot(q), lax.rem(r, NS)
        for t in range(ROWS // 512):
            cols = pl.ds(t * 512, 512)
            wacc[:, cols] += (jnp.dot(yg[q], slots[sq, :, cols], preferred_element_type=F32)
                              + jnp.dot(yg[r], slots[sr, :, cols], preferred_element_type=F32))

        @pl.when(q + NSTREAM < NH)
        def _():
            k_load(q + NSTREAM).start()

    out = pltpu.make_async_copy(wacc, w_ref, px_s)
    x_part.wait_send()
    out.start()
    v_part.wait_send()

    @pl.loop(0, last)
    def _(k):
        x_cross(k).wait_send()
        v_cross(k).wait_send()
        x_fwd(k).wait_send()
        v_fwd(k).wait_send()

    for c in (*x_last, *x_last_fwd, *v_last, *v_last_fwd, *y_last, *y_last_fwd):
        c.wait_send()

    @pl.loop(0, last)
    def _(k):
        y_part(k).wait_send()
        y_cross(k).wait_send()
        y_fwd(k).wait_send()

    y_part(last).wait_send()

    out.wait()


def solution(mesh):
    def local_program(x_loc, v_loc, length_scale, out_scale):
        dma = pltpu.SemaphoreType.DMA
        any_spec = pl.BlockSpec(memory_space=pl.ANY)
        smem = pl.BlockSpec(memory_space=pltpu.SMEM)
        out = pl.pallas_call(
            body,
            out_shape=[
                jax.ShapeDtypeStruct((COLS, ROWS), F32),
                jax.ShapeDtypeStruct((NH, CH, ROWS), BF16),
                jax.ShapeDtypeStruct((NL - NB, CH, FEAT), BF16),
                jax.ShapeDtypeStruct((NL - NB, CH, COLS), BF16),
            ],
            in_specs=[any_spec, any_spec, smem, smem],
            out_specs=[any_spec] * 4,
            scratch_shapes=[
                pltpu.VMEM((4, CH, FEAT), BF16),
                pltpu.VMEM((4, CH, COLS), BF16),
                pltpu.VMEM((FEAT, ROWS), BF16),
                pltpu.VMEM((NQ, COLS, CH), BF16),
                pltpu.VMEM((1, COLS, CH), BF16),
                pltpu.VMEM((1, CH, 128), F32),
                pltpu.VMEM((1, ROWS), F32),
                pltpu.VMEM((COLS, ROWS), F32),
                pltpu.VMEM((COLS, ROWS), F32),
                pltpu.VMEM((NS, CH, ROWS), BF16),
                dma, dma, dma, dma,
                *[dma((NB + 1,))] * 14,
                dma((2,)), dma((2,)), dma((NS,)), dma((NS,)),
            ],
            compiler_params=pltpu.CompilerParams(
                collective_id=0, has_side_effects=True, vmem_limit_bytes=67043328),
            name="two_products",
        )(x_loc.reshape(NB, CH, FEAT), v_loc.reshape(NB, CH, COLS), length_scale, out_scale)
        return out[0].T

    row_spec = P(("task", "row"), None)
    return jax.shard_map(local_program, mesh=mesh, in_specs=(row_spec, row_spec, P("task"), P("task")),
                         out_specs=row_spec, check_vma=False)
```

time: 218 us -> 208 us (0.954)
  Pallas kernels: 213 us -> 204 us
    pallas_call x1, Pallas kernels: 213 us -> 204 us  [local_program(): pl.pallas_call(body, out_shape=[jax.ShapeDtypeStruct((COLS, ROWS), F32),...]
    unnamed x1 -> x0, local copies, waits for them, and re-layouts: 3.05 us -> none
    transpose x0 -> x1, local copies, waits for them, and re-layouts: none -> 2.88 us  [local_program(): return out[0].T]
where the time goes in v2:
time: 208 us
  Pallas kernels  204 us (98%)
  local copies, waits for them, and re-layouts  2.88 us (1%)
    pallas_call x1, Pallas kernels, local_program(): pl.pallas_call(body, out_shape=[jax.ShapeDtypeStruct((COLS, ROWS), F32),...  204 us

profile of v2, /device:TPU:0, one launch (start us, length us, event | category | flops | bytes accessed | tf_op | source)
XLA Modules:
  0.0 208.1 jit_solution(13146782768093257208)
XLA Ops:
  1.3 203.9 %two_products.1 = (f32[128,4096]{1,0:T(8,128)}, bf16[24,512,4096]{2,1,0:T(8,128)(2,1)}, bf16[22,512,768]{2,1,0:T(8,128)(2,1)}, bf16[22,512,128]{2,1,0:T(8,128)(2,1)}) custom-call(bf16[8,512,768]{2,1,0:T(8,128)(2,1)} %bitcast.3, bf16[8,512,128]{2,1,0:T(8,128)(2,1)} %bitcast.5, f32[1]{0:T(128)S(6)} %copy.6.ell_ref, f32[1]{0:T(128)S(6)} %copy.7.s_ref), custom_call_target="tpu_custom_call" | custom-call | tf_op jit(solution)/shard_map/two_products/pallas_call | solution.py:362
  205.2 2.9 %copy.5 = f32[4096,128]{1,0:T(8,128)} copy(f32[4096,128]{0,1:T(8,128)} %bitcast.4) | data formatting | bytes 4194304 | tf_op jit(solution)/shard_map/transpose | solution.py:391

commit v3 on v2

--- a/solution.py
+++ b/solution.py
@@ -21,6 +21,8 @@
 TI = 256
 NT = ROWS // TI
 HALF = CH // 2
+LATE = 26
+PIECES = ((0, 256, 0, 0), (256, 128, 1, 0), (384, 128, 1, 256))
 NS = 11
 NSTREAM = 3
 NH = NQ - (NS - NSTREAM)
@@ -58,25 +60,24 @@
         return remote(vg.at[8 + 2 * k], vg.at[9 + 2 * k], fv_s.at[k], fv_r.at[k], partner)
 
     last = NB - 1
-    def halves(r, i):
-        return r.at[pl.ds(i * HALF, HALF)]
-
-    x_last = [remote(halves(x_ref.at[last], i), halves(xbuf.at[2 + i], 0), x_s.at[last + i], x_r.at[last + i], peer)
-              for i in range(2)]
-    v_last = [remote(halves(v_ref.at[last], i), halves(vbuf.at[2 + i], 0), v_s.at[last + i], v_r.at[last + i], peer)
-              for i in range(2)]
-    x_last_fwd = [remote(halves(xbuf.at[2 + i], 0), halves(xbuf.at[2 + i], 1),
-                         fx_s.at[last + i], fx_r.at[last + i], partner) for i in range(2)]
-    v_last_fwd = [remote(halves(vbuf.at[2 + i], 0), halves(vbuf.at[2 + i], 1),
-                         fv_s.at[last + i], fv_r.at[last + i], partner) for i in range(2)]
+    x_last, v_last, y_last, x_last_fwd, v_last_fwd, y_last_fwd = [], [], [], [], [], []
+    for i, (row, size, c, to) in enumerate(PIECES):
+        src, dst, fwd = pl.ds(row, size), pl.ds(to, size), pl.ds(to + size, size)
+        n = last + i
+        x_last.append(remote(x_ref.at[last, src], xbuf.at[2 + c, dst], x_s.at[n], x_r.at[n], peer))
+        v_last.append(remote(v_ref.at[last, src], vbuf.at[2 + c, dst], v_s.at[n], v_r.at[n], peer))
+        y_last.append(remote(yg.at[last, :, src], yg.at[NL + c, :, dst], yx_s.at[n], yx_r.at[n], peer))
+        x_last_fwd.append(remote(xbuf.at[2 + c, dst], xbuf.at[2 + c, fwd], fx_s.at[n], fx_r.at[n], partner))
+        v_last_fwd.append(remote(vbuf.at[2 + c, dst], vbuf.at[2 + c, fwd], fv_s.at[n], fv_r.at[n], partner))
+        y_last_fwd.append(remote(yg.at[NL + c, :, dst], yg.at[NL + c, :, fwd], yf_s.at[n], yf_r.at[n], partner))
 
     def receive_last(i):
+        x_last[i].wait_recv()
+        x_last_fwd[i].start()
         v_last[i].wait_recv()
         v_last_fwd[i].start()
-        x_last[i].wait_recv()
-        x_last_fwd[i].start()
+        x_last_fwd[i].wait_recv()
         v_last_fwd[i].wait_recv()
-        x_last_fwd[i].wait_recv()
 
     x_part = remote(x_ref, xg.at[pl.ds(0, NB)], px_s, px_r, partner)
     v_part = remote(v_ref, vg.at[pl.ds(0, NB)], pv_s, pv_r, partner)
@@ -89,14 +90,6 @@
 
     def y_fwd(k):
         return remote(yg.at[16 + 2 * k], yg.at[17 + 2 * k], yf_s.at[k], yf_r.at[k], partner)
-
-    def y_piece(k, i):
-        return yg.at[k, :, pl.ds(i * HALF, HALF)]
-
-    y_last = [remote(y_piece(last, i), y_piece(NL + i, 0), yx_s.at[last + i], yx_r.at[last + i], peer)
-              for i in range(2)]
-    y_last_fwd = [remote(y_piece(NL + i, 0), y_piece(NL + i, 1), yf_s.at[last + i], yf_r.at[last + i], partner)
-                  for i in range(2)]
 
     class Stage:
         def __init__(self, x_src, v_src, buf):
@@ -162,17 +155,19 @@
     ratio = jnp.full((8, 128), -2.0 * LOG2E, F32) / jnp.full((8, 128), 2.0 * ell * ell, F32)
     scale_e = ratio[0:1, :]
 
-    def prepare(x_i, h_i):
-        vt[h_i] = vbuf[x_i].T
-        hj[h_i] = jnp.broadcast_to(
-            0.5 * jnp.sum(jnp.square(xbuf[x_i].astype(F32)), axis=1, keepdims=True), (CH, 128))
-
-    def gen(x_i, h_i, slot, cols, width):
-        g = jnp.dot(xbuf[x_i], xt[:, cols], preferred_element_type=F32)
-        h = jnp.concatenate([hj[h_i]] * (width // 128), axis=1)
+    def prepare(x_i, rows):
+        vt[:, rows] = vbuf[x_i, rows].T
+        hj[rows] = jnp.broadcast_to(
+            0.5 * jnp.sum(jnp.square(xbuf[x_i, rows].astype(F32)), axis=1, keepdims=True), (rows.size, 128))
+
+    def gen(x_i, rows, slot, cols, width):
+        g = jnp.dot(xbuf[x_i, rows], xt[:, cols], preferred_element_type=F32)
+        h = jnp.concatenate([hj[rows]] * (width // 128), axis=1)
         c = jnp.concatenate([scale_e] * (width // 128), axis=1)
         d = jnp.maximum(h + hi[:, cols] - g, 0.0)
-        slots[slot, :, cols] = (s * jnp.exp2(d * c)).astype(BF16)
+        slots[slot, rows, cols] = (s * jnp.exp2(d * c)).astype(BF16)
+
+    every = pl.ds(0, CH)
 
     @pl.loop(0, NM)
     def _(q):
@@ -203,21 +198,25 @@
             x_part.wait_recv()
             v_part.wait_recv()
 
-        @pl.when(jnp.logical_and(n >= 16, n < NL))
-        def _():
-            @pl.when(lax.rem(n, 2) == 0)
-            def _():
-                v_cross(k).wait_recv()
-                v_fwd(k).start()
-                x_cross(k).wait_recv()
-                x_fwd(k).start()
-
-            @pl.when(lax.rem(n, 2) == 1)
-            def _():
-                v_fwd(k).wait_recv()
-                x_fwd(k).wait_recv()
-
-        @pl.when(jnp.logical_and(n >= NB, n < NL))
+        def receive():
+            v_cross(k).wait_recv()
+            v_fwd(k).start()
+            x_cross(k).wait_recv()
+            x_fwd(k).start()
+
+        from_peer = jnp.logical_and(n >= 16, lax.rem(n, 2) == 0)
+        is_late = jnp.logical_and(jnp.logical_and(from_peer, n >= LATE), n < NL)
+
+        @pl.when(jnp.logical_and(from_peer, n < LATE))
+        def _():
+            receive()
+
+        @pl.when(jnp.logical_and(jnp.logical_and(n >= 16, lax.rem(n, 2) == 1), n < NL))
+        def _():
+            v_fwd(k).wait_recv()
+            x_fwd(k).wait_recv()
+
+        @pl.when(jnp.logical_and(jnp.logical_and(n >= NB, n < NL), jnp.logical_not(is_late)))
         def _():
             stage_got(n).start()
 
@@ -230,25 +229,43 @@
             receive_last(0)
 
         x_i = jnp.where(q < NL, lax.rem(q, 2), 2)
-        prepare(x_i, 0)
+        prepare(x_i, every)
 
         def app(t):
             cols = pl.ds(t * TI, TI)
-            acc[:, cols] += jnp.dot(vt[0], slots[slot, :, cols], preferred_element_type=F32)
+            acc[:, cols] += jnp.dot(vt[...], slots[slot, :, cols], preferred_element_type=F32)
 
         for t in range(NT + 2):
             if t < NT:
-                gen(x_i, 0, slot, pl.ds(t * TI, TI), TI)
+                gen(x_i, every, slot, pl.ds(t * TI, TI), TI)
             if t >= 2:
                 app(t - 2)
 
+        @pl.when(is_late)
+        def _():
+            receive()
+            stage_got(n).start()
+
+    early, late = pl.ds(0, HALF), pl.ds(HALF, HALF)
+    slot_b = (NQ - 1) % NS
     receive_last(1)
-    prepare(3, 0)
-    slot_b = (NQ - 1) % NS
     k_out(NQ - 1 - NS).wait()
-
-    def second(q, slot):
-        for t in range(ROWS // 512):
+    prepare(3, early)
+
+    for t in range(NT):
+        gen(3, early, slot_b, pl.ds(t * TI, TI), TI)
+
+    receive_last(2)
+    prepare(3, late)
+
+    def finish(t):
+        cols = pl.ds(pl.multiple_of(t * CH, CH), CH)
+        gen(3, late, slot_b, cols, CH)
+        y = acc[:, cols] + jnp.dot(vt[...], slots[slot_b, :, cols], preferred_element_type=F32)
+        yg[t] = y.astype(BF16)
+
+    def second(q, slot, tiles=range(ROWS // 512)):
+        for t in tiles:
             cols = pl.ds(t * 512, 512)
             wacc[:, cols] += jnp.dot(yg[q], slots[slot, :, cols], preferred_element_type=F32)
 
@@ -260,62 +277,62 @@
         def _():
             k_load(q + NSTREAM).start()
 
-    @pl.loop(0, NB + 1)
+    finish(0)
+
+    @pl.loop(1, NB)
     def _(t):
-        @pl.when(t < NB)
-        def _():
-            cols = pl.ds(pl.multiple_of(t * CH, CH), CH)
-            gen(3, 0, slot_b, cols, CH)
-            y = acc[:, cols] + jnp.dot(vt[0], slots[slot_b, :, cols], preferred_element_type=F32)
-            yg[t] = y.astype(BF16)
-
-        @pl.when(t >= 1)
-        def _():
-            @pl.when(t < NB)
-            def _():
-                y_cross(t - 1).start()
-
-            @pl.when(t == NB)
-            def _():
-                y_last[0].start()
-                y_last[1].start()
-
-            y_part(t - 1).start()
-            second_streamed(t - 1)
+        y_cross(t - 1).start()
+        y_part(t - 1).start()
+        k_load(t - 1).wait()
+        finish(t)
+        second(t - 1, stream_slot(t - 1))
+        k_load(t - 1 + NSTREAM).start()
+
+    for c in y_last:
+        c.start()
+    y_part(last).start()
+    second_streamed(last)
+
+    def forward_y(k):
+        y_cross(k).wait_recv()
+        y_fwd(k).start()
 
     @pl.loop(0, NB)
     def _(i):
-        @pl.when(i < last)
-        def _():
-            y_cross(i).wait_recv()
-            y_fwd(i).start()
-
-        @pl.when(i == last)
-        def _():
-            for c, f in zip(y_last, y_last_fwd):
-                c.wait_recv()
-                f.start()
+        @pl.when(i < 3)
+        def _():
+            forward_y(i)
+
+        @pl.when(jnp.logical_or(i == 4, i == 6))
+        def _():
+            forward_y(1 + lax.div(i, 2))
 
         y_part(i).wait_recv()
         second_streamed(NB + i)
 
-    @pl.loop(0, NB)
+    @pl.loop(0, last)
     def _(i):
         q, r = 16 + i, NH + i
         k = lax.div(i, 2)
 
+        @pl.when(jnp.logical_or(i == 2, i == 3))
+        def _():
+            forward_y(3 + i)
+
+        for j in range(len(PIECES)):
+            @pl.when(i == 4 + j)
+            def _():
+                y_last[j].wait_recv()
+                y_last_fwd[j].start()
+
         @pl.when(lax.rem(i, 2) == 1)
         def _():
             y_fwd(k).wait_recv()
-
-            @pl.when(k + 4 < last)
-            def _():
-                y_fwd(k + 4).wait_recv()
+            y_fwd(k + 4).wait_recv()
 
         @pl.when(i == 6)
         def _():
-            for f in y_last_fwd:
-                f.wait_recv()
+            y_last_fwd[0].wait_recv()
 
         k_load(q).wait()
         sq, sr = stream_slot(q), lax.rem(r, NS)
@@ -328,10 +345,23 @@
         def _():
             k_load(q + NSTREAM).start()
 
-    out = pltpu.make_async_copy(wacc, w_ref, px_s)
+    y_fwd(3).wait_recv()
+    k_load(NH - 1).wait()
+    second(NH - 1, (NH - 1) % NS)
+    for f in y_last_fwd[1:]:
+        f.wait_recv()
+
+    n_out = 4
+    width = ROWS // n_out
+    outs = [pltpu.make_async_copy(wacc.at[:, pl.ds(b * width, width)], w_ref.at[:, pl.ds(b * width, width)],
+                                  kl_sem.at[b]) for b in range(n_out)]
+    for b in range(n_out):
+        second(NQ - 1, slot_b, range(b * width // 512, (b + 1) * width // 512))
+        if b:
+            outs[b - 1].start()
     x_part.wait_send()
-    out.start()
     v_part.wait_send()
+    outs[-1].start()
 
     @pl.loop(0, last)
     def _(k):
@@ -351,7 +381,8 @@
 
     y_part(last).wait_send()
 
-    out.wait()
+    for o in outs:
+        o.wait()
 
 
 def solution(mesh):
@@ -374,14 +405,14 @@
                 pltpu.VMEM((4, CH, COLS), BF16),
                 pltpu.VMEM((FEAT, ROWS), BF16),
                 pltpu.VMEM((NQ, COLS, CH), BF16),
-                pltpu.VMEM((1, COLS, CH), BF16),
-                pltpu.VMEM((1, CH, 128), F32),
+                pltpu.VMEM((COLS, CH), BF16),
+                pltpu.VMEM((CH, 128), F32),
                 pltpu.VMEM((1, ROWS), F32),
                 pltpu.VMEM((COLS, ROWS), F32),
                 pltpu.VMEM((COLS, ROWS), F32),
                 pltpu.VMEM((NS, CH, ROWS), BF16),
                 dma, dma, dma, dma,
-                *[dma((NB + 1,))] * 14,
+                *[dma((NB + len(PIECES) - 1,))] * 14,
                 dma((2,)), dma((2,)), dma((NS,)), dma((NS,)),
             ],
             compiler_params=pltpu.CompilerParams(

time: 208 us -> 201 us (0.966)
  Pallas kernels: 204 us -> 197 us
    pallas_call x1, Pallas kernels: 204 us -> 197 us  [local_program(): pl.pallas_call(body, out_shape=[jax.ShapeDtypeStruct((COLS, ROWS), F32),...]
where the time goes in v3:
time: 201 us
  Pallas kernels  197 us (98%)
  local copies, waits for them, and re-layouts  2.88 us (1%)
    pallas_call x1, Pallas kernels, local_program(): pl.pallas_call(body, out_shape=[jax.ShapeDtypeStruct((COLS, ROWS), F32),...  197 us

profile of v3, /device:TPU:0, one launch (start us, length us, event | category | flops | bytes accessed | tf_op | source)
XLA Modules:
  0.0 201.1 jit_solution(3136655804067255323)
XLA Ops:
  1.3 196.9 %two_products.1 = (f32[128,4096]{1,0:T(8,128)}, bf16[24,512,4096]{2,1,0:T(8,128)(2,1)}, bf16[22,512,768]{2,1,0:T(8,128)(2,1)}, bf16[22,512,128]{2,1,0:T(8,128)(2,1)}) custom-call(bf16[8,512,768]{2,1,0:T(8,128)(2,1)} %bitcast.3, bf16[8,512,128]{2,1,0:T(8,128)(2,1)} %bitcast.5, f32[1]{0:T(128)S(6)} %copy.6.ell_ref, f32[1]{0:T(128)S(6)} %copy.7.s_ref), custom_call_target="tpu_custom_call" | custom-call | tf_op jit(solution)/shard_map/two_products/pallas_call | solution.py:393
  198.2 2.9 %copy.5 = f32[4096,128]{1,0:T(8,128)} copy(f32[4096,128]{0,1:T(8,128)} %bitcast.4) | data formatting | bytes 4194304 | tf_op jit(solution)/shard_map/transpose | solution.py:422

commit v4 on v3

--- a/solution.py
+++ b/solution.py
@@ -264,10 +264,10 @@
         y = acc[:, cols] + jnp.dot(vt[...], slots[slot_b, :, cols], preferred_element_type=F32)
         yg[t] = y.astype(BF16)
 
-    def second(q, slot, tiles=range(ROWS // 512)):
+    def second(q, slot, tiles=range(ROWS // 512), rows=every):
         for t in tiles:
             cols = pl.ds(t * 512, 512)
-            wacc[:, cols] += jnp.dot(yg[q], slots[slot, :, cols], preferred_element_type=F32)
+            wacc[:, cols] += jnp.dot(yg[q, :, rows], slots[slot, rows, cols], preferred_element_type=F32)
 
     def second_streamed(q):
         k_load(q).wait()
@@ -346,19 +346,21 @@
             k_load(q + NSTREAM).start()
 
     y_fwd(3).wait_recv()
+    y_last_fwd[1].wait_recv()
+    second(NQ - 1, slot_b, rows=early)
+    y_last_fwd[2].wait_recv()
+    second(NQ - 1, slot_b, rows=late)
     k_load(NH - 1).wait()
-    second(NH - 1, (NH - 1) % NS)
-    for f in y_last_fwd[1:]:
-        f.wait_recv()
-
-    n_out = 4
+
+    n_out = 8
     width = ROWS // n_out
     outs = [pltpu.make_async_copy(wacc.at[:, pl.ds(b * width, width)], w_ref.at[:, pl.ds(b * width, width)],
                                   kl_sem.at[b]) for b in range(n_out)]
     for b in range(n_out):
-        second(NQ - 1, slot_b, range(b * width // 512, (b + 1) * width // 512))
+        second(NH - 1, (NH - 1) % NS, (b,))
         if b:
             outs[b - 1].start()
+
     x_part.wait_send()
     v_part.wait_send()
     outs[-1].start()

time: 201 us -> 201 us (level)
  no operation moved by 1% of the time
where the time goes in v4:
time: 201 us
  Pallas kernels  197 us (98%)
  local copies, waits for them, and re-layouts  2.88 us (1%)
    pallas_call x1, Pallas kernels, local_program(): pl.pallas_call(body, out_shape=[jax.ShapeDtypeStruct((COLS, ROWS), F32),...  197 us

profile of v4, /device:TPU:0, one launch (start us, length us, event | category | flops | bytes accessed | tf_op | source)
XLA Modules:
  0.0 201.0 jit_solution(2574564805101712192)
XLA Ops:
  1.3 196.8 %two_products.1 = (f32[128,4096]{1,0:T(8,128)}, bf16[24,512,4096]{2,1,0:T(8,128)(2,1)}, bf16[22,512,768]{2,1,0:T(8,128)(2,1)}, bf16[22,512,128]{2,1,0:T(8,128)(2,1)}) custom-call(bf16[8,512,768]{2,1,0:T(8,128)(2,1)} %bitcast.3, bf16[8,512,128]{2,1,0:T(8,128)(2,1)} %bitcast.5, f32[1]{0:T(128)S(6)} %copy.6.ell_ref, f32[1]{0:T(128)S(6)} %copy.7.s_ref), custom_call_target="tpu_custom_call" | custom-call | tf_op jit(solution)/shard_map/two_products/pallas_call | solution.py:395
  198.1 2.9 %copy.5 = f32[4096,128]{1,0:T(8,128)} copy(f32[4096,128]{0,1:T(8,128)} %bitcast.4) | data formatting | bytes 4194304 | tf_op jit(solution)/shard_map/transpose | solution.py:424
